TPU v7x, 32 devices: a whole 2x2x4 slice. The times are simulated.
32 devices in a mesh: ga: 8 (over z, y), ba: 4 (over x, core).
Axes of the slice: x: 2, y: 2, z: 4, core: 2. Of those that a mesh axis runs over, the one named last changes fastest.
Arguments:
- coefficients: bfloat16 [10240, 6144], P('ga', 'ba')
- rotation: bfloat16 [6144, 6144], P('ga', 'ba'), may hold values from -0.078125 to 0.078125
Outputs:
- new_coefficients: bfloat16 [10240, 6144], P('ga', 'ba')
- band_rms: float32 [6144], P('ba')
All inputs are finite; a program needn't handle non-finite values.
Results may differ from a plain program's by a relative error of at most 0.0004.
Values may be sent and summed in bfloat16 or wider, within the bound.
A program may use at most 128 MiB of HBM per device.

v0:
```python
import functools
import math

import jax
import jax.numpy as jnp
from jax import lax
from jax.experimental import pallas as pl
from jax.experimental.pallas import tpu as pltpu
from jax.sharding import PartitionSpec as P

MESH = pl.DeviceIdType.MESH
CHUNKS = 6
CROSS = 1


def kernel(n_ga, n_ba, line, coef, rot, total, rms_out, a_buf, b_buf, stats,
           recv, send_z, send_zb, send_y, a_recv, a_send_x, a_send_p, s_recv, s_send, own):
    lanes = n_ga // line
    depth = rot.shape[0]
    rows, width = coef.shape
    piece = depth // CHUNKS
    span = lanes * depth
    me, mb = lax.axis_index("ga"), lax.axis_index("ba")
    z, w = me // lanes, lax.rem(me, lanes)
    bx, bc = mb // 2, lax.rem(mb, 2)
    half = n_ba // 2

    def ga(i):
        return {"ga": i}

    def side(o):
        return lax.rem(w + o, lanes)

    def chunk(index):
        return b_buf.at[pl.ds(pl.multiple_of(index * piece, piece), piece)]

    partner = mb + 1 - 2 * bc
    far = [lax.rem(bx + o, half) * 2 + bc for o in range(1, half)]

    barrier = pltpu.get_barrier_semaphore()
    def greet(device):
        pl.semaphore_signal(barrier, inc=1, device_id=device, device_id_type=MESH)

    @pl.when(z > 0)
    def _():
        greet(ga(me - lanes))

    @pl.when(z < line - 1)
    def _():
        greet(ga(me + lanes))

    for o in range(1, lanes):
        greet(ga(z * lanes + side(o)))
    for target in [*far, partner]:
        greet({"ba": target})

    mine = [
        pltpu.make_async_copy(rot, b_buf.at[pl.ds(pl.multiple_of(me * depth, depth), depth)], own.at[0]),
        pltpu.make_async_copy(coef, a_buf.at[mb], own.at[1]),
    ]
    ends = (line - 1 - z) // (line - 1) + z // (line - 1)
    pl.semaphore_wait(barrier, 2 - ends + lanes - 1 + len(far) + 1)

    def remote(src, index, sem, target):
        return pltpu.make_async_remote_copy(
            src_ref=src, dst_ref=chunk(index), send_sem=sem, recv_sem=recv.at[index],
            device_id=ga(target), device_id_type=MESH)

    def arrived(index):
        pltpu.make_async_copy(chunk(index), chunk(index), recv.at[index]).wait()

    def along(k, src, index, sem):
        @pl.when(z < line - 1 if k == 0 else z > 0)
        def _():
            remote(src, index, sem, me + lanes if k == 0 else me - lanes).start()

    def across(src, index, from_z):
        for o in range(1, lanes):
            remote(src, index, send_y.at[o - 1, from_z], z * lanes + side(o)).start()

    def own_chunk(q):
        return rot.at[pl.ds(q * piece, piece)]

    last = CHUNKS - CROSS
    crossed = [(o, q) for q in range(last, CHUNKS) for o in range(1, lanes)]
    for q in range(last, CHUNKS):
        across(own_chunk(q), me * CHUNKS + q, z)
    for q in range(CHUNKS):
        for k in range(2):
            along(k, own_chunk(q), me * CHUNKS + q, send_z.at[k, z])
        if q < last:
            across(own_chunk(q), me * CHUNKS + q, z)

    def a_copy(src, index, sem, target):
        return pltpu.make_async_remote_copy(
            src_ref=src, dst_ref=a_buf.at[index], send_sem=sem, recv_sem=a_recv.at[index],
            device_id={"ba": target}, device_id_type=MESH)

    for o, target in enumerate(far):
        a_copy(coef, mb, a_send_x.at[o], target).start()
    a_copy(coef, mb, a_send_p.at[mb], partner).start()
    for copy in mine:
        copy.start()

    for o, q in crossed:
        index = (z * lanes + side(o)) * CHUNKS + q
        arrived(index)
        for k in range(2):
            along(k, chunk(index), index, send_zb.at[k, z * lanes + side(o)])

    tile = math.gcd(rows, 1280)

    def multiply(j, dist, part):
        from_z = z - dist + 2 * dist * j

        @pl.when((from_z >= 0) & (from_z < line) & ((dist > 0) | (j == 0)))
        def _():
            if part == "all":
                for o in range(1, lanes):
                    for q in range(last):
                        arrived((from_z * lanes + side(o)) * CHUNKS + q)
                panel(from_z * span, span, dist)
                return
            if part == "own":
                panel((from_z * lanes + w) * depth, depth, dist)
                return
            for o in range(1, lanes):
                block = from_z * lanes + side(o)
                for q in range(cut) if part == "cut" else range(cut, last):
                    arrived(block * CHUNKS + q)
                if part == "cut":
                    panel(block * depth, cut * piece, dist)
                else:
                    panel(block * depth + cut * piece, depth - cut * piece, dist)

    cut = max(q for q in range(last) if q * piece % 128 == 0) if depth % 128 == 0 else 0

    def panel(begin, size, dist):
        at, column = begin // width, pl.multiple_of(lax.rem(begin, width), 128)

        @pl.loop(0, rows // tile)
        def _(t):
            part = pl.ds(pl.multiple_of(t * tile, tile), tile)
            product = jnp.dot(
                a_buf[at, part, pl.ds(column, size)],
                b_buf[pl.ds(pl.multiple_of(begin, 128), size), :],
                preferred_element_type=jnp.float32)

            @pl.when(dist == 0)
            def _():
                total[part, :] = product

            @pl.when(dist > 0)
            def _():
                total[part, :] += product

    def at_distance(dist, part="all"):
        if cut == 0:
            if part in ("own", "cut"):
                return
            part = "all"
        lax.fori_loop(0, 2, lambda j, c: (multiply(j, dist, part), c)[1], 0)

    def relay(d, carry):
        for step, (o, q) in enumerate([(0, q) for q in range(CHUNKS)] + crossed):
            for k in range(2):
                from_z = z - d if k == 0 else z + d

                @pl.when((from_z >= 0) & (from_z < line))
                def _():
                    block = from_z * lanes + side(o)
                    index = block * CHUNKS + q
                    arrived(index)
                    along(k, chunk(index), index, send_zb.at[k, block] if o else send_z.at[k, from_z])
                    if q < last:
                        across(chunk(index), index, from_z)

            if step == CHUNKS // 3:
                @pl.when(d == 2)
                def _():
                    for source in far:
                        pltpu.make_async_copy(a_buf.at[source], a_buf.at[source], a_recv.at[source]).wait()
                        a_copy(a_buf.at[source], source, a_send_p.at[source], partner).start()

            if step == CHUNKS // 6:
                @pl.when(d == line - 1)
                def _():
                    at_distance(line - 3)

            for when, dist, part in ((CHUNKS // 2, line - 2, "own"), (CHUNKS - 2, line - 2, "cut"),
                                     (CHUNKS - 2, line - 2, "rest"), (CHUNKS - 1, line - 1, "own"),
                                     (CHUNKS - 1, line - 1, "cut")):
                if step == when:
                    @pl.when(d == line - 1)
                    def _():
                        at_distance(dist, part)

            if step == CHUNKS - 1:
                @pl.when(d == 2)
                def _():
                    for copy in mine:
                        copy.wait()
                    for x in range(half):
                        source = x * 2 + 1 - bc
                        pltpu.make_async_copy(a_buf.at[source], a_buf.at[source], a_recv.at[source]).wait()

                @pl.when((d >= 2) & (d < line - 1))
                def _():
                    at_distance(d - 2)
        return carry

    lax.fori_loop(1, line, relay, 0)
    at_distance(line - 1, "rest")

    def squares(t, c):
        v = total[pl.ds(pl.multiple_of(t * tile, tile), tile), :]
        return c + jnp.sum(v * v, axis=0, keepdims=True)

    stats[me] = lax.fori_loop(0, rows // tile, squares, jnp.zeros((1, total.shape[1]), jnp.float32))

    def share(o, target, slot):
        return pltpu.make_async_remote_copy(
            src_ref=stats.at[me], dst_ref=stats.at[me], send_sem=s_send.at[o], recv_sem=s_recv.at[slot],
            device_id=ga(target), device_id_type=MESH)

    for o in range(1, n_ga):
        share(o, lax.rem(me + o, n_ga), me).start()
    for o in range(1, n_ga):
        source = lax.rem(me + o, n_ga)
        pltpu.make_async_copy(stats.at[source], stats.at[source], s_recv.at[source]).wait()
    everything = stats[0]
    for g in range(1, n_ga):
        everything = everything + stats[g]
    rms = jnp.sqrt(everything / (rows * n_ga) + 1e-06)
    rms_out[...] = rms
    for o in range(1, n_ga):
        share(o, lax.rem(me + o, n_ga), me).wait_send()
    for o, target in enumerate(far):
        a_copy(coef, mb, a_send_x.at[o], target).wait_send()
    for x in range(half):
        a_copy(coef, x * 2 + bc, a_send_p.at[x * 2 + bc], partner).wait_send()

    def sent(count, sem):
        view = b_buf.at[pl.ds(0, count * piece)]
        pltpu.make_async_copy(view, view, sem).wait()

    for from_z in range(line):
        for k in range(2):
            @pl.when((z >= from_z) & (z < line - 1) if k == 0 else (z <= from_z) & (z > 0))
            def _():
                sent(CHUNKS, send_z.at[k, from_z])
                for o in range(1, lanes):
                    sent(CROSS, send_zb.at[k, from_z * lanes + side(o)])
        for o in range(1, lanes):
            @pl.when(z == from_z)
            def _():
                sent(CHUNKS, send_y.at[o - 1, from_z])

            @pl.when(z != from_z)
            def _():
                sent(last, send_y.at[o - 1, from_z])


def solution(mesh):
    n_ga, n_ba = mesh.shape["ga"], mesh.shape["ba"]
    line = 2 ** math.ceil(math.log2(n_ga) / 2)
    lanes = n_ga // line

    def body(coef, rot):
        rows, width = coef.shape
        depth, columns = rot.shape
        dma = pltpu.SemaphoreType.DMA
        rotated, rms = pl.pallas_call(
            functools.partial(kernel, n_ga, n_ba, line),
            out_shape=(pltpu.VMEM((rows, columns), jnp.float32),
                       pltpu.VMEM((1, columns), jnp.float32)),
            in_specs=[pl.BlockSpec(memory_space=pltpu.HBM)] * 2,
            out_specs=(pl.BlockSpec(memory_space=pltpu.VMEM),) * 2,
            scratch_shapes=[
                pltpu.VMEM((n_ba, rows, width), jnp.bfloat16),
                pltpu.VMEM((n_ga * depth, columns), jnp.bfloat16),
                pltpu.VMEM((n_ga, 1, columns), jnp.float32),
                dma((n_ga * CHUNKS,)),
                dma((2, line)),
                dma((2, n_ga)),
                dma((lanes - 1, line)),
                dma((n_ba,)),
                dma((n_ba // 2 - 1,)),
                dma((n_ba,)),
                dma((n_ga,)),
                dma((n_ga,)),
                dma((2,)),
            ],
            compiler_params=pltpu.CompilerParams(
                collective_id=0, has_side_effects=True, vmem_limit_bytes=48 * 2**20),
        )(*(pltpu.with_memory_space_constraint(x, pltpu.HBM) for x in (coef, rot)))
        return (rotated * (1.0 / rms)).astype(jnp.bfloat16), rms.reshape(columns)

    return jax.shard_map(body, mesh=mesh, in_specs=(P("ga", "ba"), P("ga", "ba")),
                         out_specs=(P("ga", "ba"), P("ba")), check_vma=False)
```

profile of v0, /device:TPU:0, one launch (start us, length us, event | category | flops | bytes accessed | tf_op | source)
XLA Modules:
  0.0 194.3 jit_solution(10132732712249216167)
XLA Ops:
  0.6 190.1 %shard_map.41 = (f32[1280,1536]{1,0:T(8,128)S(1)}, f32[1,1536]{1,0:T(1,128)S(1)}) custom-call(bf16[1280,1536]{1,0:T(8,128)(2,1)} %coef.1, bf16[768,1536]{1,0:T(8,128)(2,1)} %rot.1), custom_call_target="tpu_custom_call" | custom-call | tf_op jit(solution)/shard_map/pallas_call | solution.py:273
  190.8 0.6 fusion
  191.4 2.9 %multiply_convert_fusion = bf16[1280,1536]{1,0:T(8,128)(2,1)} fusion(f32[1280,1536]{1,0:T(8,128)S(1)} %get-tuple-element.4, f32[1536]{0:T(1024)S(1)} %get-tuple-element.7), kind=kLoop, calls=%fused_computation | loop fusion | flops 3932160 | bytes 11802624 | tf_op jit(solution)/shard_map/convert_element_type | solution.py:297
where the time goes:
time: 194 us
  Pallas kernels  190 us (98%)
  other arithmetic  3.56 us (2%)
    pallas_call x1, Pallas kernels, body(): pl.pallas_call(functools.partial(kernel, n_ga, n_ba, line), out_shape=(pl...  190 us

commit v1 on v0

--- a/solution.py
+++ b/solution.py
@@ -11,6 +11,7 @@
 MESH = pl.DeviceIdType.MESH
 CHUNKS = 6
 CROSS = 1
+LENT = 6
 
 
 def kernel(n_ga, n_ba, line, coef, rot, total, rms_out, a_buf, b_buf, stats,
@@ -261,38 +262,494 @@
                 sent(last, send_y.at[o - 1, from_z])
 
 
+PIECES = 12
+GIVEN = 10
+
+
+def edge_kernel(n_ga, n_ba, line, lent, coef, rot, total, rms_out, a_buf, c_buf, b_buf, f_buf, l_buf, stats,
+                recv, send_z, send_zb, send_y, f_recv, f_send, f_cross, a_recv, a_send_x, a_send_p,
+                c_recv, c_send, l_recv, l_send, s_recv, s_send, own):
+    lanes = n_ga // line
+    depth = rot.shape[0]
+    rows, width = coef.shape
+    kept = rot.shape[1] - lent
+    piece = depth // PIECES
+    given = rows // GIVEN
+    last = PIECES - 1
+    half = rows // 2
+    me, mb = lax.axis_index("ga"), lax.axis_index("ba")
+    z, w = me // lanes, lax.rem(me, lanes)
+    v = 1 - w
+    bx, bc = mb // 2, lax.rem(mb, 2)
+    partner = mb + 1 - 2 * bc
+    far = (1 - bx) * 2 + bc
+    beyond = (1 - bx) * 2 + 1 - bc
+    inside = lax.rem((z + 1) // 2, 2)
+    upper = z // (line // 2)
+    mate = z + 1 - 2 * lax.rem(z, 2)
+    toward = z + 1 - 2 * upper
+    skip = upper * (line - 1)
+    sx, sc = skip // 2, lax.rem(skip, 2)
+    crosses = bc + sc - 2 * bc * sc
+    late = (1 - crosses) * (1 - bx - sx + 2 * bx * sx)
+    entry = mb + late * (far - mb)
+
+    def ga(i):
+        return {"ga": i}
+
+    def ba(i):
+        return {"ba": i}
+
+    def remote(src, dst, send, arrive, target):
+        return pltpu.make_async_remote_copy(
+            src_ref=src, dst_ref=dst, send_sem=send, recv_sem=arrive, device_id=target, device_id_type=MESH)
+
+    def landed(ref, sem):
+        pltpu.make_async_copy(ref, ref, sem).wait()
+
+    barrier = pltpu.get_barrier_semaphore()
+    def greet(device):
+        pl.semaphore_signal(barrier, inc=1, device_id=device, device_id_type=MESH)
+
+    @pl.when(z > 0)
+    def _():
+        greet(ga(me - lanes))
+
+    @pl.when(z < line - 1)
+    def _():
+        greet(ga(me + lanes))
+
+    greet(ga(z * lanes + v))
+    greet(ba(far))
+    greet(ba(partner))
+
+    mine = [
+        pltpu.make_async_copy(
+            rot.at[:, pl.ds(lent, kept)], b_buf.at[pl.ds(pl.multiple_of(me * depth, depth), depth)], own.at[0]),
+        pltpu.make_async_copy(
+            rot.at[:, pl.ds(0, lent)], f_buf.at[pl.ds(pl.multiple_of(me * depth, depth), depth)], own.at[1]),
+        pltpu.make_async_copy(coef, a_buf.at[mb], own.at[2]),
+    ]
+    ends = (line - 1 - z) // (line - 1) + z // (line - 1)
+    pl.semaphore_wait(barrier, 2 - ends + 3)
+
+    def chunk(index):
+        return b_buf.at[pl.ds(pl.multiple_of(index * piece, piece), piece)]
+
+    def arrived(index):
+        landed(chunk(index), recv.at[index])
+
+    def along(k, src, index, sem):
+        @pl.when(z < line - 1 if k == 0 else z > 0)
+        def _():
+            remote(src, chunk(index), sem, recv.at[index], ga(me + lanes if k == 0 else me - lanes)).start()
+
+    def across(src, index, from_z):
+        remote(src, chunk(index), send_y.at[from_z], recv.at[index], ga(z * lanes + v)).start()
+
+    def own_chunk(q):
+        return rot.at[pl.ds(q * piece, piece), pl.ds(lent, kept)]
+
+    def f_block(block):
+        return f_buf.at[pl.ds(pl.multiple_of(block * depth, depth), depth)]
+
+    def f_arrived(block):
+        landed(f_block(block), f_recv.at[block])
+
+    def f_along(src, block):
+        remote(src, f_block(block), f_send.at[block], f_recv.at[block], ga(toward * lanes + w)).start()
+
+    f_own = rot.at[:, pl.ds(0, lent)]
+    f_over = remote(f_own, f_block(me), f_cross.at[0], f_recv.at[me], ga(z * lanes + v))
+    f_over.start()
+    across(own_chunk(last), me * PIECES + last, z)
+    f_along(f_own, me)
+    for q in range(PIECES):
+        for k in range(2):
+            along(k, own_chunk(q), me * PIECES + q, send_z.at[k, z])
+        if q < last:
+            across(own_chunk(q), me * PIECES + q, z)
+
+    def a_copy(src, index, sem, target):
+        return remote(src, a_buf.at[index], sem, a_recv.at[index], ba(target))
+
+    a_copy(coef, mb, a_send_x.at[0], far).start()
+    a_copy(coef, mb, a_send_p.at[0], partner).start()
+    for copy in mine:
+        copy.start()
+
+    total[...] = jnp.zeros_like(total)
+    side = z * lanes + v
+    f_arrived(side)
+    f_along(f_block(side), side)
+    arrived(side * PIECES + last)
+    for k in range(2):
+        along(k, chunk(side * PIECES + last), side * PIECES + last, send_zb.at[k, side])
+
+    def strip(r):
+        return pl.ds(pl.multiple_of(r * given, given), given)
+
+    def c_at(block, r):
+        return c_buf.at[block - 1 + upper, strip(r)]
+
+    def c_copy(src, block, r, sem, target):
+        return remote(src, c_at(block, r), sem, c_recv.at[block, r], target)
+
+    def lend(source):
+        @pl.loop(0, GIVEN)
+        def _(r):
+            c_copy(source.at[strip(r)], entry, r, c_send.at[0], ga(mate * lanes + w)).start()
+
+    @pl.when((inside == 0) & (late == 0))
+    def _():
+        lend(coef)
+
+    @pl.when(inside == 1)
+    def _():
+        f_arrived(mate * lanes + w)
+        f_along(f_block(mate * lanes + w), mate * lanes + w)
+
+    def pass_entry(r):
+        landed(c_at(entry, r), c_recv.at[entry, r])
+
+        @pl.when(crosses == 1)
+        def _():
+            c_copy(c_at(entry, r), entry, r, c_send.at[1], ba(far)).start()
+
+        c_copy(c_at(entry, r), entry, r, c_send.at[2], ba(partner)).start()
+
+    def pass_far(r):
+        @pl.when(crosses == 1)
+        def _():
+            landed(c_at(far, r), c_recv.at[far, r])
+            c_copy(c_at(far, r), far, r, c_send.at[3], ba(partner)).start()
+
+    def ready():
+        for copy in mine:
+            copy.wait()
+        for source in (partner, beyond):
+            landed(a_buf.at[source], a_recv.at[source])
+
+    def order(i):
+        j, lane = i // lanes, lax.rem(i, lanes)
+        near = j + inside * (1 - j // 2) * (1 - 2 * lax.rem(j, 2))
+        from_z = near + upper * (line - 1 - 2 * near)
+        return from_z * lanes + w + lane * (1 - 2 * w), lane
+
+    def panel(begin, size):
+        at, column = begin // width, pl.multiple_of(lax.rem(begin, width), 128)
+
+        @pl.loop(0, 2)
+        def _(t):
+            part = pl.ds(pl.multiple_of(t * half, half), half)
+            total[part, pl.ds(lent, kept)] += jnp.dot(
+                a_buf[at, part, pl.ds(column, size)],
+                b_buf[pl.ds(pl.multiple_of(begin, 128), size), :],
+                preferred_element_type=jnp.float32)
+
+    def crossing(block, begin, end):
+        @pl.loop(begin, end)
+        def _(q):
+            arrived(block * PIECES + q)
+
+    def whole(i):
+        block, lane = order(i)
+
+        @pl.when(lane == 1)
+        def _():
+            crossing(block, 0, last)
+
+        panel(block * depth, depth)
+
+    steps = PIECES + 1
+
+    @pl.loop(0, (line - 1) * steps)
+    def _(t):
+        d, step = 1 + t // steps, lax.rem(t, steps)
+        crossed = step // PIECES
+        q = step - crossed
+
+        @pl.when((inside == 1) & (d == 1) & (step == last))
+        def _():
+            f_arrived(mate * lanes + v)
+            f_along(f_block(mate * lanes + v), mate * lanes + v)
+
+        for k in range(2):
+            from_z = z - d if k == 0 else z + d
+
+            @pl.when((from_z >= 0) & (from_z < line))
+            def _():
+                @pl.when(crossed == 0)
+                def _():
+                    index = (from_z * lanes + w) * PIECES + q
+                    arrived(index)
+                    along(k, chunk(index), index, send_z.at[k, from_z])
+
+                    @pl.when(q < last)
+                    def _():
+                        across(chunk(index), index, from_z)
+
+                @pl.when(crossed == 1)
+                def _():
+                    block = from_z * lanes + v
+                    index = block * PIECES + q
+                    arrived(index)
+                    along(k, chunk(index), index, send_zb.at[k, block])
+
+        @pl.when((d == 2) & (step == inside * 4 + (1 - inside) * PIECES))
+        def _():
+            landed(a_buf.at[far], a_recv.at[far])
+            a_copy(a_buf.at[far], far, a_send_p.at[1], partner).start()
+
+            @pl.when((inside == 0) & (late == 1))
+            def _():
+                lend(a_buf.at[far])
+
+        @pl.when((inside == 1) & (d == 2) & (lax.rem(step, 2) == 1))
+        def _():
+            r = step // 2
+
+            @pl.when(late == 0)
+            def _():
+                pass_entry(r)
+
+            @pl.when(r >= 3)
+            def _():
+                pass_far(r - 3)
+
+        turn = step - inside * 6 - (1 - inside) * 2
+
+        @pl.when((d == 3 - inside) & (turn >= 0) & (turn < 8) & (lax.rem(turn + 8, 2) == 0))
+        def _():
+            n = turn // 2
+
+            @pl.when(n == 0)
+            def _():
+                ready()
+
+            whole(n + n // 3)
+
+    def lent_product(source, part, begin, count):
+        product = jnp.dot(
+            source[0, part, :], f_buf[pl.ds(begin, width), :], preferred_element_type=jnp.float32)
+        for s in range(1, count):
+            product += jnp.dot(
+                source[s, part, :], f_buf[pl.ds(begin + s * width, width), :], preferred_element_type=jnp.float32)
+        return product
+
+    @pl.when(inside == 1)
+    def _():
+        for from_z in (toward, toward + 1 - 2 * lax.rem(toward, 2)):
+            for lane in range(lanes):
+                f_arrived(from_z * lanes + lane)
+
+        @pl.when(late == 1)
+        def _():
+            pass_entry(0)
+            pass_entry(1)
+
+    @pl.loop(0, GIVEN)
+    def _(r):
+        @pl.when(inside == 1)
+        def _():
+            @pl.when(late == 1)
+            def _():
+                @pl.when(r + 2 < GIVEN)
+                def _():
+                    pass_entry(r + 2)
+
+            @pl.when(late == 0)
+            def _():
+                for when, which in ((0, 6), (1, 7), (4, 8), (6, 9)):
+                    @pl.when(r == when)
+                    def _():
+                        pass_entry(which)
+
+            @pl.when(r < 4)
+            def _():
+                pass_far(3 + r)
+
+            @pl.when(r >= 7)
+            def _():
+                pass_far(r)
+
+            @pl.when(crosses == 1)
+            def _():
+                given_block = (1 - sx) * 2 + sc
+                landed(c_at(given_block, r), c_recv.at[given_block, r])
+
+            @pl.when(crosses == 0)
+            def _():
+                for source in (partner, beyond):
+                    landed(c_at(source, r), c_recv.at[source, r])
+
+            l_buf[strip(r), :] = lent_product(
+                c_buf, strip(r), pl.multiple_of((1 - upper) * width, width), n_ba - 1)
+            remote(l_buf.at[strip(r)], l_buf.at[strip(r)], l_send.at[0], l_recv.at[r], ga(mate * lanes + w)).start()
+
+        @pl.when(r < 3)
+        def _():
+            whole(6 - r * 3 + r // 2 * 5)
+
+        @pl.when((r == 3) | (r == 4))
+        def _():
+            part = pl.ds(pl.multiple_of((r - 3) * half, half), half)
+
+            @pl.when(inside == 1)
+            def _():
+                total[part, pl.ds(0, lent)] = lent_product(a_buf, part, 0, n_ba)
+
+            @pl.when(inside == 0)
+            def _():
+                total[part, pl.ds(0, lent)] = jnp.dot(
+                    a_buf[skip, part, :], f_buf[pl.ds(pl.multiple_of(skip * width, width), width), :],
+                    preferred_element_type=jnp.float32)
+
+    final, _ = order(7)
+    cut = last * piece // 256 * 256
+    crossing(final, 0, cut // piece)
+    panel(final * depth, cut)
+
+    @pl.when(inside == 0)
+    def _():
+        @pl.loop(0, GIVEN)
+        def _(r):
+            landed(l_buf.at[strip(r)], l_recv.at[r])
+            total[strip(r), pl.ds(0, lent)] += l_buf[strip(r), :]
+
+    crossing(final, cut // piece, last)
+    panel(final * depth + cut, depth - cut)
+
+    v_all = total[...]
+    stats[me] = jnp.sum(v_all * v_all, axis=0, keepdims=True)
+
+    def share(o, target, slot):
+        return remote(stats.at[me], stats.at[me], s_send.at[o], s_recv.at[slot], ga(target))
+
+    for o in range(1, n_ga):
+        share(o, lax.rem(me + o, n_ga), me).start()
+
+    a_copy(coef, mb, a_send_x.at[0], far).wait_send()
+    for i in range(2):
+        a_copy(coef, mb, a_send_p.at[i], partner).wait_send()
+
+    def sent(count, sem):
+        landed(b_buf.at[pl.ds(0, count * piece)], sem)
+
+    f_over.wait_send()
+    for lane in range(lanes):
+        block = z * lanes + lane
+        landed(f_block(block), f_send.at[block])
+
+    @pl.when(inside == 0)
+    def _():
+        landed(c_buf.at[0], c_send.at[0])
+
+    @pl.when(inside == 1)
+    def _():
+        for lane in range(lanes):
+            block = mate * lanes + lane
+            landed(f_block(block), f_send.at[block])
+        landed(c_buf.at[0], c_send.at[2])
+        landed(l_buf, l_send.at[0])
+
+        @pl.when(crosses == 1)
+        def _():
+            landed(c_buf.at[0], c_send.at[1])
+            landed(c_buf.at[0], c_send.at[3])
+
+    for from_z in range(line):
+        for k in range(2):
+            @pl.when((z >= from_z) & (z < line - 1) if k == 0 else (z <= from_z) & (z > 0))
+            def _():
+                sent(PIECES, send_z.at[k, from_z])
+                sent(1, send_zb.at[k, from_z * lanes + v])
+
+        @pl.when(z == from_z)
+        def _():
+            sent(PIECES, send_y.at[from_z])
+
+        @pl.when(z != from_z)
+        def _():
+            sent(last, send_y.at[from_z])
+
+    for o in range(1, n_ga):
+        source = lax.rem(me + o, n_ga)
+        landed(stats.at[source], s_recv.at[source])
+    everything = stats[0]
+    for g in range(1, n_ga):
+        everything = everything + stats[g]
+    rms_out[...] = jnp.sqrt(everything / (rows * n_ga) + 1e-06)
+    for o in range(1, n_ga):
+        share(o, lax.rem(me + o, n_ga), me).wait_send()
+
+
 def solution(mesh):
     n_ga, n_ba = mesh.shape["ga"], mesh.shape["ba"]
     line = 2 ** math.ceil(math.log2(n_ga) / 2)
     lanes = n_ga // line
 
+    def edges(rows, width, depth, columns):
+        dma = pltpu.SemaphoreType.DMA
+        lent = columns // LENT // 128 * 128
+        return functools.partial(edge_kernel, n_ga, n_ba, line, lent), [
+            pltpu.VMEM((n_ba, rows, width), jnp.bfloat16),
+            pltpu.VMEM((n_ba - 1, rows, width), jnp.bfloat16),
+            pltpu.VMEM((n_ga * depth, columns - lent), jnp.bfloat16),
+            pltpu.VMEM((n_ga * depth, lent), jnp.bfloat16),
+            pltpu.VMEM((rows, lent), jnp.float32),
+            pltpu.VMEM((n_ga, 1, columns), jnp.float32),
+            dma((n_ga * PIECES,)),
+            dma((2, line)),
+            dma((2, n_ga)),
+            dma((line,)),
+            dma((n_ga,)),
+            dma((n_ga,)),
+            dma((1,)),
+            dma((n_ba,)),
+            dma((1,)),
+            dma((2,)),
+            dma((n_ba, GIVEN)),
+            dma((4,)),
+            dma((GIVEN,)),
+            dma((1,)),
+            dma((n_ga,)),
+            dma((n_ga,)),
+            dma((3,)),
+        ], 56 * 2**20
+
+    def plain(rows, width, depth, columns):
+        dma = pltpu.SemaphoreType.DMA
+        return functools.partial(kernel, n_ga, n_ba, line), [
+            pltpu.VMEM((n_ba, rows, width), jnp.bfloat16),
+            pltpu.VMEM((n_ga * depth, columns), jnp.bfloat16),
+            pltpu.VMEM((n_ga, 1, columns), jnp.float32),
+            dma((n_ga * CHUNKS,)),
+            dma((2, line)),
+            dma((2, n_ga)),
+            dma((lanes - 1, line)),
+            dma((n_ba,)),
+            dma((n_ba // 2 - 1,)),
+            dma((n_ba,)),
+            dma((n_ga,)),
+            dma((n_ga,)),
+            dma((2,)),
+        ], 48 * 2**20
+
     def body(coef, rot):
         rows, width = coef.shape
         depth, columns = rot.shape
-        dma = pltpu.SemaphoreType.DMA
+        build = edges if (line, lanes, n_ba) == (4, 2, 4) else plain
+        run, scratch, limit = build(rows, width, depth, columns)
         rotated, rms = pl.pallas_call(
-            functools.partial(kernel, n_ga, n_ba, line),
+            run,
             out_shape=(pltpu.VMEM((rows, columns), jnp.float32),
                        pltpu.VMEM((1, columns), jnp.float32)),
             in_specs=[pl.BlockSpec(memory_space=pltpu.HBM)] * 2,
             out_specs=(pl.BlockSpec(memory_space=pltpu.VMEM),) * 2,
-            scratch_shapes=[
-                pltpu.VMEM((n_ba, rows, width), jnp.bfloat16),
-                pltpu.VMEM((n_ga * depth, columns), jnp.bfloat16),
-                pltpu.VMEM((n_ga, 1, columns), jnp.float32),
-                dma((n_ga * CHUNKS,)),
-                dma((2, line)),
-                dma((2, n_ga)),
-                dma((lanes - 1, line)),
-                dma((n_ba,)),
-                dma((n_ba // 2 - 1,)),
-                dma((n_ba,)),
-                dma((n_ga,)),
-                dma((n_ga,)),
-                dma((2,)),
-            ],
+            scratch_shapes=scratch,
             compiler_params=pltpu.CompilerParams(
-                collective_id=0, has_side_effects=True, vmem_limit_bytes=48 * 2**20),
+                collective_id=0, has_side_effects=True, vmem_limit_bytes=limit),
         )(*(pltpu.with_memory_space_constraint(x, pltpu.HBM) for x in (coef, rot)))
         return (rotated * (1.0 / rms)).astype(jnp.bfloat16), rms.reshape(columns)
 

time: 194 us -> 185 us (0.954)
  Pallas kernels: 190 us -> 181 us
    pallas_call x1, Pallas kernels: 190 us -> 181 us  [body(): pl.pallas_call(run, out_shape=(pltpu.VMEM((rows, columns), jnp.float32),...]
where the time goes in v1:
time: 185 us
  Pallas kernels  181 us (98%)
  other arithmetic  3.56 us (2%)
    pallas_call x1, Pallas kernels, body(): pl.pallas_call(run, out_shape=(pltpu.VMEM((rows, columns), jnp.float32),...  181 us

profile of v1, /device:TPU:0, one launch (start us, length us, event | category | flops | bytes accessed | tf_op | source)
XLA Modules:
  0.0 184.8 jit_solution(6604006922522105630)
XLA Ops:
  0.6 180.6 %shard_map.41 = (f32[1280,1536]{1,0:T(8,128)S(1)}, f32[1,1536]{1,0:T(1,128)S(1)}) custom-call(bf16[1280,1536]{1,0:T(8,128)(2,1)} %coef.1, bf16[768,1536]{1,0:T(8,128)(2,1)} %rot.1), custom_call_target="tpu_custom_call" | custom-call | tf_op jit(solution)/shard_map/pallas_call | solution.py:744
  181.3 0.6 fusion
  181.9 2.9 %multiply_convert_fusion = bf16[1280,1536]{1,0:T(8,128)(2,1)} fusion(f32[1280,1536]{1,0:T(8,128)S(1)} %get-tuple-element.4, f32[1536]{0:T(1024)S(1)} %get-tuple-element.7), kind=kLoop, calls=%fused_computation | loop fusion | flops 3932160 | bytes 11802624 | tf_op jit(solution)/shard_map/convert_element_type | solution.py:754

commit v2 on v1

--- a/solution.py
+++ b/solution.py
@@ -266,8 +266,8 @@
 GIVEN = 10
 
 
-def edge_kernel(n_ga, n_ba, line, lent, coef, rot, total, rms_out, a_buf, c_buf, b_buf, f_buf, l_buf, stats,
-                recv, send_z, send_zb, send_y, f_recv, f_send, f_cross, a_recv, a_send_x, a_send_p,
+def edge_kernel(n_ga, n_ba, line, lent, coef, rot, out, rms_out, total, a_buf, c_buf, b_buf, f_buf, l_buf, stats,
+                recv, recv_y, recv_x, send_z, send_y, f_recv, f_send, a_recv, a_send,
                 c_recv, c_send, l_recv, l_send, s_recv, s_send, own):
     lanes = n_ga // line
     depth = rot.shape[0]
@@ -336,16 +336,23 @@
     def chunk(index):
         return b_buf.at[pl.ds(pl.multiple_of(index * piece, piece), piece)]
 
-    def arrived(index):
-        landed(chunk(index), recv.at[index])
-
-    def along(k, src, index, sem):
+    cut = last * piece // 256 * 256
+    early = cut // piece
+
+    def along(k, src, index, arrive):
         @pl.when(z < line - 1 if k == 0 else z > 0)
         def _():
-            remote(src, chunk(index), sem, recv.at[index], ga(me + lanes if k == 0 else me - lanes)).start()
-
-    def across(src, index, from_z):
-        remote(src, chunk(index), send_y.at[from_z], recv.at[index], ga(z * lanes + v)).start()
+            remote(src, chunk(index), send_z.at[k], arrive, ga(me + lanes if k == 0 else me - lanes)).start()
+
+    def across(src, from_z, q):
+        index = (from_z * lanes + w) * PIECES + q
+        slot = from_z * 2 + q // early
+        remote(src, chunk(index), send_y.at[0], recv_y.at[slot], ga(z * lanes + v)).start()
+
+    def crossed_over(block, part):
+        begin, count = (0, early) if part == 0 else (early, last - early)
+        view = b_buf.at[pl.ds(pl.multiple_of(block * depth + begin * piece, piece), count * piece)]
+        landed(view, recv_y.at[block // lanes * 2 + part])
 
     def own_chunk(q):
         return rot.at[pl.ds(q * piece, piece), pl.ds(lent, kept)]
@@ -353,38 +360,39 @@
     def f_block(block):
         return f_buf.at[pl.ds(pl.multiple_of(block * depth, depth), depth)]
 
-    def f_arrived(block):
-        landed(f_block(block), f_recv.at[block])
-
-    def f_along(src, block):
-        remote(src, f_block(block), f_send.at[block], f_recv.at[block], ga(toward * lanes + w)).start()
+    def f_arrived(block, slot):
+        landed(f_block(block), f_recv.at[slot])
+
+    def f_along(src, block, slot):
+        remote(src, f_block(block), f_send.at[0], f_recv.at[slot + inside * (3 - slot)], ga(toward * lanes + w)).start()
 
     f_own = rot.at[:, pl.ds(0, lent)]
-    f_over = remote(f_own, f_block(me), f_cross.at[0], f_recv.at[me], ga(z * lanes + v))
+    f_over = remote(f_own, f_block(me), f_send.at[1], f_recv.at[0], ga(z * lanes + v))
     f_over.start()
-    across(own_chunk(last), me * PIECES + last, z)
-    f_along(f_own, me)
+    over = remote(own_chunk(last), chunk(me * PIECES + last), send_y.at[1], recv_x.at[z], ga(z * lanes + v))
+    over.start()
+    f_along(f_own, me, 1)
     for q in range(PIECES):
         for k in range(2):
-            along(k, own_chunk(q), me * PIECES + q, send_z.at[k, z])
+            along(k, own_chunk(q), me * PIECES + q, recv.at[z * PIECES + q])
         if q < last:
-            across(own_chunk(q), me * PIECES + q, z)
+            across(own_chunk(q), z, q)
 
     def a_copy(src, index, sem, target):
         return remote(src, a_buf.at[index], sem, a_recv.at[index], ba(target))
 
-    a_copy(coef, mb, a_send_x.at[0], far).start()
-    a_copy(coef, mb, a_send_p.at[0], partner).start()
+    a_copy(coef, mb, a_send.at[0], far).start()
+    a_copy(coef, mb, a_send.at[1], partner).start()
     for copy in mine:
         copy.start()
 
     total[...] = jnp.zeros_like(total)
     side = z * lanes + v
-    f_arrived(side)
-    f_along(f_block(side), side)
-    arrived(side * PIECES + last)
+    f_arrived(side, 0)
+    f_along(f_block(side), side, 2)
+    landed(chunk(side * PIECES + last), recv_x.at[z])
     for k in range(2):
-        along(k, chunk(side * PIECES + last), side * PIECES + last, send_zb.at[k, side])
+        along(k, chunk(side * PIECES + last), side * PIECES + last, recv_x.at[z])
 
     def strip(r):
         return pl.ds(pl.multiple_of(r * given, given), given)
@@ -392,13 +400,13 @@
     def c_at(block, r):
         return c_buf.at[block - 1 + upper, strip(r)]
 
-    def c_copy(src, block, r, sem, target):
-        return remote(src, c_at(block, r), sem, c_recv.at[block, r], target)
+    def c_copy(src, block, r, kind, sem, target):
+        return remote(src, c_at(block, r), c_send.at[sem], c_recv.at[kind * GIVEN + r], target)
 
     def lend(source):
         @pl.loop(0, GIVEN)
         def _(r):
-            c_copy(source.at[strip(r)], entry, r, c_send.at[0], ga(mate * lanes + w)).start()
+            c_copy(source.at[strip(r)], entry, r, 0, 0, ga(mate * lanes + w)).start()
 
     @pl.when((inside == 0) & (late == 0))
     def _():
@@ -406,23 +414,23 @@
 
     @pl.when(inside == 1)
     def _():
-        f_arrived(mate * lanes + w)
-        f_along(f_block(mate * lanes + w), mate * lanes + w)
+        f_arrived(mate * lanes + w, 1)
+        f_along(f_block(mate * lanes + w), mate * lanes + w, 3)
 
     def pass_entry(r):
-        landed(c_at(entry, r), c_recv.at[entry, r])
+        landed(c_at(entry, r), c_recv.at[r])
 
         @pl.when(crosses == 1)
         def _():
-            c_copy(c_at(entry, r), entry, r, c_send.at[1], ba(far)).start()
-
-        c_copy(c_at(entry, r), entry, r, c_send.at[2], ba(partner)).start()
+            c_copy(c_at(entry, r), entry, r, 1, 1, ba(far)).start()
+
+        c_copy(c_at(entry, r), entry, r, 2, 2, ba(partner)).start()
 
     def pass_far(r):
         @pl.when(crosses == 1)
         def _():
-            landed(c_at(far, r), c_recv.at[far, r])
-            c_copy(c_at(far, r), far, r, c_send.at[3], ba(partner)).start()
+            landed(c_at(far, r), c_recv.at[GIVEN + r])
+            c_copy(c_at(far, r), far, r, 2, 2, ba(partner)).start()
 
     def ready():
         for copy in mine:
@@ -447,17 +455,13 @@
                 b_buf[pl.ds(pl.multiple_of(begin, 128), size), :],
                 preferred_element_type=jnp.float32)
 
-    def crossing(block, begin, end):
-        @pl.loop(begin, end)
-        def _(q):
-            arrived(block * PIECES + q)
-
     def whole(i):
         block, lane = order(i)
 
         @pl.when(lane == 1)
         def _():
-            crossing(block, 0, last)
+            crossed_over(block, 0)
+            crossed_over(block, 1)
 
         panel(block * depth, depth)
 
@@ -471,8 +475,8 @@
 
         @pl.when((inside == 1) & (d == 1) & (step == last))
         def _():
-            f_arrived(mate * lanes + v)
-            f_along(f_block(mate * lanes + v), mate * lanes + v)
+            f_arrived(mate * lanes + v, 2)
+            f_along(f_block(mate * lanes + v), mate * lanes + v, 3)
 
         for k in range(2):
             from_z = z - d if k == 0 else z + d
@@ -482,24 +486,24 @@
                 @pl.when(crossed == 0)
                 def _():
                     index = (from_z * lanes + w) * PIECES + q
-                    arrived(index)
-                    along(k, chunk(index), index, send_z.at[k, from_z])
+                    sem = recv.at[from_z * PIECES + q]
+                    landed(chunk(index), sem)
+                    along(k, chunk(index), index, sem)
 
                     @pl.when(q < last)
                     def _():
-                        across(chunk(index), index, from_z)
+                        across(chunk(index), from_z, q)
 
                 @pl.when(crossed == 1)
                 def _():
-                    block = from_z * lanes + v
-                    index = block * PIECES + q
-                    arrived(index)
-                    along(k, chunk(index), index, send_zb.at[k, block])
+                    index = (from_z * lanes + v) * PIECES + last
+                    landed(chunk(index), recv_x.at[from_z])
+                    along(k, chunk(index), index, recv_x.at[from_z])
 
         @pl.when((d == 2) & (step == inside * 4 + (1 - inside) * PIECES))
         def _():
             landed(a_buf.at[far], a_recv.at[far])
-            a_copy(a_buf.at[far], far, a_send_p.at[1], partner).start()
+            a_copy(a_buf.at[far], far, a_send.at[1], partner).start()
 
             @pl.when((inside == 0) & (late == 1))
             def _():
@@ -539,9 +543,7 @@
 
     @pl.when(inside == 1)
     def _():
-        for from_z in (toward, toward + 1 - 2 * lax.rem(toward, 2)):
-            for lane in range(lanes):
-                f_arrived(from_z * lanes + lane)
+        landed(f_buf.at[pl.ds(0, 2 * lanes * depth)], f_recv.at[3])
 
         @pl.when(late == 1)
         def _():
@@ -575,17 +577,15 @@
 
             @pl.when(crosses == 1)
             def _():
-                given_block = (1 - sx) * 2 + sc
-                landed(c_at(given_block, r), c_recv.at[given_block, r])
+                landed(c_at((1 - sx) * 2 + sc, r), c_recv.at[2 * GIVEN + r])
 
             @pl.when(crosses == 0)
             def _():
-                for source in (partner, beyond):
-                    landed(c_at(source, r), c_recv.at[source, r])
+                landed(c_buf.at[pl.ds(0, 2), strip(r)], c_recv.at[2 * GIVEN + r])
 
             l_buf[strip(r), :] = lent_product(
                 c_buf, strip(r), pl.multiple_of((1 - upper) * width, width), n_ba - 1)
-            remote(l_buf.at[strip(r)], l_buf.at[strip(r)], l_send.at[0], l_recv.at[r], ga(mate * lanes + w)).start()
+            remote(l_buf.at[strip(r)], l_buf.at[strip(r)], l_send.at[0], l_recv.at[0], ga(mate * lanes + w)).start()
 
         @pl.when(r < 3)
         def _():
@@ -606,82 +606,89 @@
                     preferred_element_type=jnp.float32)
 
     final, _ = order(7)
-    cut = last * piece // 256 * 256
-    crossing(final, 0, cut // piece)
+    crossed_over(final, 0)
     panel(final * depth, cut)
 
     @pl.when(inside == 0)
     def _():
-        @pl.loop(0, GIVEN)
-        def _(r):
-            landed(l_buf.at[strip(r)], l_recv.at[r])
-            total[strip(r), pl.ds(0, lent)] += l_buf[strip(r), :]
-
-    crossing(final, cut // piece, last)
-    panel(final * depth + cut, depth - cut)
-
-    v_all = total[...]
-    stats[me] = jnp.sum(v_all * v_all, axis=0, keepdims=True)
-
-    def share(o, target, slot):
-        return remote(stats.at[me], stats.at[me], s_send.at[o], s_recv.at[slot], ga(target))
-
-    for o in range(1, n_ga):
-        share(o, lax.rem(me + o, n_ga), me).start()
-
-    a_copy(coef, mb, a_send_x.at[0], far).wait_send()
-    for i in range(2):
-        a_copy(coef, mb, a_send_p.at[i], partner).wait_send()
+        landed(l_buf, l_recv.at[0])
+        total[:, pl.ds(0, lent)] += l_buf[...]
+
+    lent_part = total[:, pl.ds(0, lent)]
+    stats[me, :, pl.ds(0, lent)] = jnp.sum(lent_part * lent_part, axis=0, keepdims=True)
+    crossed_over(final, 1)
+    begin = final * depth + cut
+    at, column = begin // width, pl.multiple_of(lax.rem(begin, width), 128)
+
+    def finish(t, squares):
+        part = pl.ds(pl.multiple_of(t * half, half), half)
+        done = total[part, pl.ds(lent, kept)] + jnp.dot(
+            a_buf[at, part, pl.ds(column, depth - cut)],
+            b_buf[pl.ds(pl.multiple_of(begin, 128), depth - cut), :],
+            preferred_element_type=jnp.float32)
+        total[part, pl.ds(lent, kept)] = done
+        return squares + jnp.sum(done * done, axis=0, keepdims=True)
+
+    stats[me, :, pl.ds(lent, kept)] = lax.fori_loop(0, 2, finish, jnp.zeros((1, kept), jnp.float32))
+
+    def share(target):
+        return remote(stats.at[me], stats.at[me], s_send.at[0], s_recv.at[0], ga(target))
+
+    planes = (line - 1 - z, lax.rem(z + line // 2, line), mate)
+    others = [plane * lanes + lane for plane in planes for lane in (v, w)] + [z * lanes + v]
+    for target in others:
+        share(target).start()
 
     def sent(count, sem):
         landed(b_buf.at[pl.ds(0, count * piece)], sem)
 
+    landed(a_buf.at[0], a_send.at[0])
+    landed(a_buf.at[pl.ds(0, 2)], a_send.at[1])
     f_over.wait_send()
-    for lane in range(lanes):
-        block = z * lanes + lane
-        landed(f_block(block), f_send.at[block])
+    over.wait_send()
 
     @pl.when(inside == 0)
     def _():
+        landed(f_buf.at[pl.ds(0, lanes * depth)], f_send.at[0])
         landed(c_buf.at[0], c_send.at[0])
 
     @pl.when(inside == 1)
     def _():
-        for lane in range(lanes):
-            block = mate * lanes + lane
-            landed(f_block(block), f_send.at[block])
-        landed(c_buf.at[0], c_send.at[2])
+        landed(f_buf.at[pl.ds(0, 2 * lanes * depth)], f_send.at[0])
         landed(l_buf, l_send.at[0])
 
         @pl.when(crosses == 1)
         def _():
             landed(c_buf.at[0], c_send.at[1])
-            landed(c_buf.at[0], c_send.at[3])
-
-    for from_z in range(line):
-        for k in range(2):
-            @pl.when((z >= from_z) & (z < line - 1) if k == 0 else (z <= from_z) & (z > 0))
-            def _():
-                sent(PIECES, send_z.at[k, from_z])
-                sent(1, send_zb.at[k, from_z * lanes + v])
-
-        @pl.when(z == from_z)
-        def _():
-            sent(PIECES, send_y.at[from_z])
-
-        @pl.when(z != from_z)
-        def _():
-            sent(last, send_y.at[from_z])
-
-    for o in range(1, n_ga):
-        source = lax.rem(me + o, n_ga)
-        landed(stats.at[source], s_recv.at[source])
+            landed(c_buf.at[pl.ds(0, 2)], c_send.at[2])
+
+        @pl.when(crosses == 0)
+        def _():
+            landed(c_buf.at[0], c_send.at[2])
+
+    for plane in range(line):
+        @pl.when(z == plane)
+        def _():
+            if plane < line - 1:
+                sent((plane + 1) * steps, send_z.at[0])
+            if plane > 0:
+                sent((line - plane) * steps, send_z.at[1])
+
+    sent(line * last, send_y.at[0])
+    landed(stats.at[pl.ds(0, n_ga - 1)], s_recv.at[0])
     everything = stats[0]
     for g in range(1, n_ga):
         everything = everything + stats[g]
-    rms_out[...] = jnp.sqrt(everything / (rows * n_ga) + 1e-06)
-    for o in range(1, n_ga):
-        share(o, lax.rem(me + o, n_ga), me).wait_send()
+    rms = jnp.sqrt(everything / (rows * n_ga) + 1e-06)
+    rms_out[...] = rms
+    scale = 1.0 / rms
+
+    @pl.loop(0, 2)
+    def _(t):
+        part = pl.ds(pl.multiple_of(t * half, half), half)
+        out[part, :] = (total[part, :] * scale).astype(jnp.bfloat16)
+
+    landed(stats.at[pl.ds(0, n_ga - 1)], s_send.at[0])
 
 
 def solution(mesh):
@@ -693,30 +700,30 @@
         dma = pltpu.SemaphoreType.DMA
         lent = columns // LENT // 128 * 128
         return functools.partial(edge_kernel, n_ga, n_ba, line, lent), [
+            pltpu.VMEM((rows, columns), jnp.float32),
             pltpu.VMEM((n_ba, rows, width), jnp.bfloat16),
             pltpu.VMEM((n_ba - 1, rows, width), jnp.bfloat16),
             pltpu.VMEM((n_ga * depth, columns - lent), jnp.bfloat16),
             pltpu.VMEM((n_ga * depth, lent), jnp.bfloat16),
             pltpu.VMEM((rows, lent), jnp.float32),
             pltpu.VMEM((n_ga, 1, columns), jnp.float32),
-            dma((n_ga * PIECES,)),
-            dma((2, line)),
-            dma((2, n_ga)),
+            dma((line * PIECES,)),
+            dma((2 * line,)),
             dma((line,)),
-            dma((n_ga,)),
-            dma((n_ga,)),
+            dma((2,)),
+            dma((2,)),
+            dma((4,)),
+            dma((2,)),
+            dma((n_ba,)),
+            dma((2,)),
+            dma((3 * GIVEN,)),
+            dma((3,)),
             dma((1,)),
-            dma((n_ba,)),
             dma((1,)),
-            dma((2,)),
-            dma((n_ba, GIVEN)),
-            dma((4,)),
-            dma((GIVEN,)),
             dma((1,)),
-            dma((n_ga,)),
-            dma((n_ga,)),
+            dma((1,)),
             dma((3,)),
-        ], 56 * 2**20
+        ], 59 * 2**20
 
     def plain(rows, width, depth, columns):
         dma = pltpu.SemaphoreType.DMA
@@ -739,11 +746,11 @@
     def body(coef, rot):
         rows, width = coef.shape
         depth, columns = rot.shape
-        build = edges if (line, lanes, n_ba) == (4, 2, 4) else plain
-        run, scratch, limit = build(rows, width, depth, columns)
+        lends = (line, lanes, n_ba) == (4, 2, 4)
+        run, scratch, limit = (edges if lends else plain)(rows, width, depth, columns)
         rotated, rms = pl.pallas_call(
             run,
-            out_shape=(pltpu.VMEM((rows, columns), jnp.float32),
+            out_shape=(pltpu.VMEM((rows, columns), jnp.bfloat16 if lends else jnp.float32),
                        pltpu.VMEM((1, columns), jnp.float32)),
             in_specs=[pl.BlockSpec(memory_space=pltpu.HBM)] * 2,
             out_specs=(pl.BlockSpec(memory_space=pltpu.VMEM),) * 2,
@@ -751,7 +758,9 @@
             compiler_params=pltpu.CompilerParams(
                 collective_id=0, has_side_effects=True, vmem_limit_bytes=limit),
         )(*(pltpu.with_memory_space_constraint(x, pltpu.HBM) for x in (coef, rot)))
-        return (rotated * (1.0 / rms)).astype(jnp.bfloat16), rms.reshape(columns)
+        if not lends:
+            rotated = (rotated * (1.0 / rms)).astype(jnp.bfloat16)
+        return rotated, rms.reshape(columns)
 
     return jax.shard_map(body, mesh=mesh, in_specs=(P("ga", "ba"), P("ga", "ba")),
                          out_specs=(P("ga", "ba"), P("ba")), check_vma=False)

time: 185 us -> 183 us (0.989)
  other arithmetic: 3.56 us -> 0.62 us
  local copies, waits for them, and re-layouts: 0 us -> 1.93 us
    convert_element_type x1 -> x0, other arithmetic: 2.93 us -> none  [body(): return ((rotated * (1.0 / rms)).astype(jnp.bfloat16), rms.reshape(columns))]
    unnamed x0 -> x1, local copies, waits for them, and re-layouts: none -> 1.93 us
where the time goes in v2:
time: 183 us
  Pallas kernels  180 us (98%)
  local copies, waits for them, and re-layouts  1.93 us (1%)
    pallas_call x1, Pallas kernels, body(): pl.pallas_call(run, out_shape=(pltpu.VMEM((rows, columns), jnp.bfloat16 i...  180 us

profile of v2, /device:TPU:0, one launch (start us, length us, event | category | flops | bytes accessed | tf_op | source)
XLA Modules:
  0.0 182.8 jit_solution(4417892747070556358)
XLA Ops:
  0.6 179.7 %shard_map.41 = (bf16[1280,1536]{1,0:T(8,128)(2,1)S(1)}, f32[1,1536]{1,0:T(1,128)S(1)}) custom-call(bf16[1280,1536]{1,0:T(8,128)(2,1)} %coef.1, bf16[768,1536]{1,0:T(8,128)(2,1)} %rot.1), custom_call_target="tpu_custom_call" | custom-call | tf_op jit(solution)/shard_map/pallas_call | solution.py:751
  180.3 1.9 %copy.5 = bf16[1280,1536]{1,0:T(8,128)(2,1)} copy(bf16[1280,1536]{1,0:T(8,128)(2,1)S(1)} %get-tuple-element.6) | data formatting | bytes 7864320
  182.2 0.6 reduce

commit v3 on v2

--- a/solution.py
+++ b/solution.py
@@ -12,6 +12,7 @@
 CHUNKS = 6
 CROSS = 1
 LENT = 6
+MORE = 12
 
 
 def kernel(n_ga, n_ba, line, coef, rot, total, rms_out, a_buf, b_buf, stats,
@@ -263,16 +264,18 @@
 
 
 PIECES = 12
-GIVEN = 10
-
-
-def edge_kernel(n_ga, n_ba, line, lent, coef, rot, out, rms_out, total, a_buf, c_buf, b_buf, f_buf, l_buf, stats,
+GIVEN = 20
+
+
+def edge_kernel(n_ga, n_ba, line, widths, coef, rot, out, rms_out, total, a_buf, c_buf, b_buf, f_buf, g_buf, l_buf, m_buf, stats,
                 recv, recv_y, recv_x, send_z, send_y, f_recv, f_send, a_recv, a_send,
                 c_recv, c_send, l_recv, l_send, s_recv, s_send, own):
     lanes = n_ga // line
     depth = rot.shape[0]
     rows, width = coef.shape
+    lent = sum(widths)
     kept = rot.shape[1] - lent
+    groups = ((f_buf, l_buf, 0, widths[0]), (g_buf, m_buf, widths[0], widths[1]))
     piece = depth // PIECES
     given = rows // GIVEN
     last = PIECES - 1
@@ -326,9 +329,11 @@
     mine = [
         pltpu.make_async_copy(
             rot.at[:, pl.ds(lent, kept)], b_buf.at[pl.ds(pl.multiple_of(me * depth, depth), depth)], own.at[0]),
+        pltpu.make_async_copy(coef, a_buf.at[mb], own.at[1]),
+    ] + [
         pltpu.make_async_copy(
-            rot.at[:, pl.ds(0, lent)], f_buf.at[pl.ds(pl.multiple_of(me * depth, depth), depth)], own.at[1]),
-        pltpu.make_async_copy(coef, a_buf.at[mb], own.at[2]),
+            rot.at[:, pl.ds(begin, size)], held.at[pl.ds(pl.multiple_of(me * depth, depth), depth)], own.at[2 + g])
+        for g, (held, _, begin, size) in enumerate(groups)
     ]
     ends = (line - 1 - z) // (line - 1) + z // (line - 1)
     pl.semaphore_wait(barrier, 2 - ends + 3)
@@ -350,28 +355,48 @@
         remote(src, chunk(index), send_y.at[0], recv_y.at[slot], ga(z * lanes + v)).start()
 
     def crossed_over(block, part):
-        begin, count = (0, early) if part == 0 else (early, last - early)
-        view = b_buf.at[pl.ds(pl.multiple_of(block * depth + begin * piece, piece), count * piece)]
-        landed(view, recv_y.at[block // lanes * 2 + part])
+        def wait(begin, end):
+            view = b_buf.at[pl.ds(pl.multiple_of(block * depth + begin * piece, piece), (end - begin) * piece)]
+            landed(view, recv_y.at[block // lanes * 2 + part])
+
+        if part == 0:
+            wait(0, early)
+            return
+        gap = (z - block // lanes) * (z - block // lanes)
+
+        @pl.when(gap < 2)
+        def _():
+            wait(early, last)
+
+        @pl.when(gap >= 2)
+        def _():
+            wait(early, PIECES)
 
     def own_chunk(q):
         return rot.at[pl.ds(q * piece, piece), pl.ds(lent, kept)]
 
-    def f_block(block):
-        return f_buf.at[pl.ds(pl.multiple_of(block * depth, depth), depth)]
-
-    def f_arrived(block, slot):
-        landed(f_block(block), f_recv.at[slot])
-
-    def f_along(src, block, slot):
-        remote(src, f_block(block), f_send.at[0], f_recv.at[slot + inside * (3 - slot)], ga(toward * lanes + w)).start()
-
-    f_own = rot.at[:, pl.ds(0, lent)]
-    f_over = remote(f_own, f_block(me), f_send.at[1], f_recv.at[0], ga(z * lanes + v))
-    f_over.start()
+    def f_block(g, block):
+        return groups[g][0].at[pl.ds(pl.multiple_of(block * depth, depth), depth)]
+
+    def f_arrived(g, block, slot):
+        landed(f_block(g, block), f_recv.at[4 * g + slot])
+
+    def f_along(g, src, block, slot):
+        arrive = f_recv.at[4 * g + slot + inside * (3 - slot)]
+        remote(src, f_block(g, block), f_send.at[g], arrive, ga(toward * lanes + w)).start()
+
+    def f_pass(g, block, slot, later):
+        f_arrived(g, block, slot)
+        f_along(g, f_block(g, block), block, later)
+
+    f_own = [rot.at[:, pl.ds(begin, size)] for _, _, begin, size in groups]
+    f_over = [
+        remote(f_own[g], f_block(g, me), f_send.at[2 + g], f_recv.at[4 * g], ga(z * lanes + v)) for g in range(2)]
+    f_over[0].start()
     over = remote(own_chunk(last), chunk(me * PIECES + last), send_y.at[1], recv_x.at[z], ga(z * lanes + v))
     over.start()
-    f_along(f_own, me, 1)
+    f_over[1].start()
+    f_along(0, f_own[0], me, 1)
     for q in range(PIECES):
         for k in range(2):
             along(k, own_chunk(q), me * PIECES + q, recv.at[z * PIECES + q])
@@ -388,8 +413,7 @@
 
     total[...] = jnp.zeros_like(total)
     side = z * lanes + v
-    f_arrived(side, 0)
-    f_along(f_block(side), side, 2)
+    f_pass(0, side, 0, 2)
     landed(chunk(side * PIECES + last), recv_x.at[z])
     for k in range(2):
         along(k, chunk(side * PIECES + last), side * PIECES + last, recv_x.at[z])
@@ -408,14 +432,21 @@
         def _(r):
             c_copy(source.at[strip(r)], entry, r, 0, 0, ga(mate * lanes + w)).start()
 
+    def second():
+        f_along(1, f_own[1], me, 1)
+        f_pass(1, side, 0, 2)
+
+    @pl.when(inside == 0)
+    def _():
+        second()
+
     @pl.when((inside == 0) & (late == 0))
     def _():
         lend(coef)
 
     @pl.when(inside == 1)
     def _():
-        f_arrived(mate * lanes + w, 1)
-        f_along(f_block(mate * lanes + w), mate * lanes + w, 3)
+        f_pass(0, mate * lanes + w, 1, 3)
 
     def pass_entry(r):
         landed(c_at(entry, r), c_recv.at[r])
@@ -431,6 +462,10 @@
         def _():
             landed(c_at(far, r), c_recv.at[GIVEN + r])
             c_copy(c_at(far, r), far, r, 2, 2, ba(partner)).start()
+
+    def both(job, r):
+        job(2 * r)
+        job(2 * r + 1)
 
     def ready():
         for copy in mine:
@@ -473,10 +508,15 @@
         crossed = step // PIECES
         q = step - crossed
 
-        @pl.when((inside == 1) & (d == 1) & (step == last))
-        def _():
-            f_arrived(mate * lanes + v, 2)
-            f_along(f_block(mate * lanes + v), mate * lanes + v, 3)
+        @pl.when((inside == 1) & (d == 1) & (step == PIECES))
+        def _():
+            f_pass(0, mate * lanes + v, 2, 3)
+
+        @pl.when((inside == 1) & (d == 2) & (step == 0))
+        def _():
+            second()
+            f_pass(1, mate * lanes + w, 1, 3)
+            f_pass(1, mate * lanes + v, 2, 3)
 
         for k in range(2):
             from_z = z - d if k == 0 else z + d
@@ -490,15 +530,13 @@
                     landed(chunk(index), sem)
                     along(k, chunk(index), index, sem)
 
-                    @pl.when(q < last)
+                    @pl.when((q < last) | (d > 1))
                     def _():
                         across(chunk(index), from_z, q)
 
-                @pl.when(crossed == 1)
+                @pl.when((crossed == 1) & (d == 1))
                 def _():
-                    index = (from_z * lanes + v) * PIECES + last
-                    landed(chunk(index), recv_x.at[from_z])
-                    along(k, chunk(index), index, recv_x.at[from_z])
+                    landed(chunk((from_z * lanes + v) * PIECES + last), recv_x.at[from_z])
 
         @pl.when((d == 2) & (step == inside * 4 + (1 - inside) * PIECES))
         def _():
@@ -509,21 +547,21 @@
             def _():
                 lend(a_buf.at[far])
 
-        @pl.when((inside == 1) & (d == 2) & (lax.rem(step, 2) == 1))
-        def _():
-            r = step // 2
+        @pl.when((inside == 1) & (d == 2) & (step > 2) & (step < 10) & (lax.rem(step, 2) == 1))
+        def _():
+            r = step // 2 - 1
 
             @pl.when(late == 0)
             def _():
-                pass_entry(r)
+                both(pass_entry, r)
 
             @pl.when(r >= 3)
             def _():
-                pass_far(r - 3)
+                both(pass_far, r - 3)
 
         turn = step - inside * 6 - (1 - inside) * 2
 
-        @pl.when((d == 3 - inside) & (turn >= 0) & (turn < 8) & (lax.rem(turn + 8, 2) == 0))
+        @pl.when((d == 3 - inside) & (turn >= 0) & (turn < 6) & (lax.rem(turn + 8, 2) == 0))
         def _():
             n = turn // 2
 
@@ -531,79 +569,130 @@
             def _():
                 ready()
 
-            whole(n + n // 3)
-
-    def lent_product(source, part, begin, count):
+            whole(n)
+
+    def lent_product(source, part, held, begin, count):
         product = jnp.dot(
-            source[0, part, :], f_buf[pl.ds(begin, width), :], preferred_element_type=jnp.float32)
+            source[0, part, :], held[pl.ds(begin, width), :], preferred_element_type=jnp.float32)
         for s in range(1, count):
             product += jnp.dot(
-                source[s, part, :], f_buf[pl.ds(begin + s * width, width), :], preferred_element_type=jnp.float32)
+                source[s, part, :], held[pl.ds(begin + s * width, width), :], preferred_element_type=jnp.float32)
         return product
 
+    def answer(g, r, count=2):
+        held, back, _, _ = groups[g]
+        part = pl.ds(pl.multiple_of(r * count * given, given), count * given)
+        back[part, :] = lent_product(
+            c_buf, part, held, pl.multiple_of((1 - upper) * width, width), n_ba - 1)
+        remote(back.at[part], back.at[part], l_send.at[g], l_recv.at[g], ga(mate * lanes + w)).start()
+
+    def joined(r):
+        both(joined_half, r)
+
+    def joined_half(r):
+        @pl.when(crosses == 1)
+        def _():
+            landed(c_at((1 - sx) * 2 + sc, r), c_recv.at[2 * GIVEN + r])
+
+        @pl.when(crosses == 0)
+        def _():
+            landed(c_buf.at[pl.ds(0, 2), strip(r)], c_recv.at[2 * GIVEN + r])
+
+    def serve(at, prompt=(), slow=(), distant=()):
+        for condition, jobs, job in ((late == 0, prompt, pass_entry), (late == 1, slow, pass_entry), (True, distant, pass_far)):
+            for when, which in jobs:
+                @pl.when((at == when) & condition)
+                def _():
+                    both(job, which)
+
+    def all_here(g):
+        landed(groups[g][0].at[pl.ds(0, 2 * lanes * depth)], f_recv.at[4 * g + 3])
+
+    def own_lent(g):
+        held, _, begin, size = groups[g]
+
+        def compute(t):
+            part = pl.ds(pl.multiple_of(t * half, half), half)
+            total[part, pl.ds(begin, size)] = lent_product(a_buf, part, held, 0, n_ba)
+        return compute
+
+    @pl.loop(0, 4)
+    def _(j):
+        @pl.when((inside == 1) & (j == 1))
+        def _():
+            serve(j, prompt=((1, 4),), distant=((1, 1), (1, 2)))
+
+        @pl.when((inside == 1) & (j == 2))
+        def _():
+            all_here(0)
+
+            @pl.loop(0, 4)
+            def _(r):
+                serve(r, slow=((0, 0), (1, 1), (2, 2), (3, 3)), distant=((0, 3), (1, 4)))
+                joined(r)
+                answer(0, r)
+
+            serve(j, prompt=((2, 5),))
+            pl.loop(0, 2)(own_lent(0))
+
+        @pl.when((inside == 1) & (j >= 2))
+        def _():
+            serve(j, prompt=((2, 6), (3, 7)), slow=((2, 4), (3, 5)), distant=((2, 5), (3, 6)))
+            joined(j + 2)
+            answer(0, j + 2)
+
+            @pl.when(j == 2)
+            def _():
+                all_here(1)
+
+            @pl.loop(4 * j - 8, 2 * j)
+            def _(r):
+                answer(1, r)
+
+            @pl.when(j == 3)
+            def _():
+                serve(j, slow=((3, 6),))
+                joined(6)
+                answer(0, 6)
+                answer(1, 6)
+                pl.loop(0, 2)(own_lent(1))
+                serve(j, prompt=((3, 8),), slow=((3, 7),), distant=((3, 7),))
+
+        whole(4 + 2 * j - j // 2 * 5)
+
+    @pl.when(inside == 0)
+    def _():
+        for held, _, begin, size in groups:
+            @pl.loop(0, 2)
+            def _(t):
+                part = pl.ds(pl.multiple_of(t * half, half), half)
+                total[part, pl.ds(begin, size)] = jnp.dot(
+                    a_buf[skip, part, :], held[pl.ds(pl.multiple_of(skip * width, width), width), :],
+                    preferred_element_type=jnp.float32)
+
     @pl.when(inside == 1)
     def _():
-        landed(f_buf.at[pl.ds(0, 2 * lanes * depth)], f_recv.at[3])
-
-        @pl.when(late == 1)
-        def _():
-            pass_entry(0)
-            pass_entry(1)
-
-    @pl.loop(0, GIVEN)
-    def _(r):
-        @pl.when(inside == 1)
-        def _():
-            @pl.when(late == 1)
-            def _():
-                @pl.when(r + 2 < GIVEN)
-                def _():
-                    pass_entry(r + 2)
-
-            @pl.when(late == 0)
-            def _():
-                for when, which in ((0, 6), (1, 7), (4, 8), (6, 9)):
-                    @pl.when(r == when)
-                    def _():
-                        pass_entry(which)
-
-            @pl.when(r < 4)
-            def _():
-                pass_far(3 + r)
-
-            @pl.when(r >= 7)
-            def _():
-                pass_far(r)
-
-            @pl.when(crosses == 1)
-            def _():
-                landed(c_at((1 - sx) * 2 + sc, r), c_recv.at[2 * GIVEN + r])
-
-            @pl.when(crosses == 0)
-            def _():
-                landed(c_buf.at[pl.ds(0, 2), strip(r)], c_recv.at[2 * GIVEN + r])
-
-            l_buf[strip(r), :] = lent_product(
-                c_buf, strip(r), pl.multiple_of((1 - upper) * width, width), n_ba - 1)
-            remote(l_buf.at[strip(r)], l_buf.at[strip(r)], l_send.at[0], l_recv.at[0], ga(mate * lanes + w)).start()
-
-        @pl.when(r < 3)
-        def _():
-            whole(6 - r * 3 + r // 2 * 5)
-
-        @pl.when((r == 3) | (r == 4))
-        def _():
-            part = pl.ds(pl.multiple_of((r - 3) * half, half), half)
-
-            @pl.when(inside == 1)
-            def _():
-                total[part, pl.ds(0, lent)] = lent_product(a_buf, part, 0, n_ba)
-
-            @pl.when(inside == 0)
-            def _():
-                total[part, pl.ds(0, lent)] = jnp.dot(
-                    a_buf[skip, part, :], f_buf[pl.ds(pl.multiple_of(skip * width, width), width), :],
-                    preferred_element_type=jnp.float32)
+        @pl.loop(7, 9)
+        def _(r):
+            serve(r, slow=((7, 8),))
+
+            @pl.when(r == 8)
+            def _():
+                pass_entry(18)
+
+            serve(r, distant=((8, 8),))
+            joined(r)
+            answer(0, r)
+            answer(1, r)
+
+        pass_entry(19)
+
+        @pl.loop(18, 20)
+        def _(r):
+            pass_far(r)
+            joined_half(r)
+            answer(0, r, 1)
+            answer(1, r, 1)
 
     final, _ = order(7)
     crossed_over(final, 0)
@@ -611,8 +700,9 @@
 
     @pl.when(inside == 0)
     def _():
-        landed(l_buf, l_recv.at[0])
-        total[:, pl.ds(0, lent)] += l_buf[...]
+        for g, (_, back, begin, size) in enumerate(groups):
+            landed(back, l_recv.at[g])
+            total[:, pl.ds(begin, size)] += back[...]
 
     lent_part = total[:, pl.ds(0, lent)]
     stats[me, :, pl.ds(0, lent)] = jnp.sum(lent_part * lent_part, axis=0, keepdims=True)
@@ -644,18 +734,21 @@
 
     landed(a_buf.at[0], a_send.at[0])
     landed(a_buf.at[pl.ds(0, 2)], a_send.at[1])
-    f_over.wait_send()
+    for g in range(2):
+        f_over[g].wait_send()
     over.wait_send()
 
     @pl.when(inside == 0)
     def _():
-        landed(f_buf.at[pl.ds(0, lanes * depth)], f_send.at[0])
+        for g in range(2):
+            landed(groups[g][0].at[pl.ds(0, lanes * depth)], f_send.at[g])
         landed(c_buf.at[0], c_send.at[0])
 
     @pl.when(inside == 1)
     def _():
-        landed(f_buf.at[pl.ds(0, 2 * lanes * depth)], f_send.at[0])
-        landed(l_buf, l_send.at[0])
+        for g in range(2):
+            landed(groups[g][0].at[pl.ds(0, 2 * lanes * depth)], f_send.at[g])
+            landed(groups[g][1], l_send.at[g])
 
         @pl.when(crosses == 1)
         def _():
@@ -670,11 +763,11 @@
         @pl.when(z == plane)
         def _():
             if plane < line - 1:
-                sent((plane + 1) * steps, send_z.at[0])
+                sent((plane + 1) * PIECES + 1, send_z.at[0])
             if plane > 0:
-                sent((line - plane) * steps, send_z.at[1])
-
-    sent(line * last, send_y.at[0])
+                sent((line - plane) * PIECES + 1, send_z.at[1])
+            sent(line * last + sum(abs(plane - other) > 1 for other in range(line)), send_y.at[0])
+
     landed(stats.at[pl.ds(0, n_ga - 1)], s_recv.at[0])
     everything = stats[0]
     for g in range(1, n_ga):
@@ -698,31 +791,31 @@
 
     def edges(rows, width, depth, columns):
         dma = pltpu.SemaphoreType.DMA
-        lent = columns // LENT // 128 * 128
-        return functools.partial(edge_kernel, n_ga, n_ba, line, lent), [
+        widths = columns // LENT // 128 * 128, columns // MORE // 128 * 128
+        return functools.partial(edge_kernel, n_ga, n_ba, line, widths), [
             pltpu.VMEM((rows, columns), jnp.float32),
             pltpu.VMEM((n_ba, rows, width), jnp.bfloat16),
             pltpu.VMEM((n_ba - 1, rows, width), jnp.bfloat16),
-            pltpu.VMEM((n_ga * depth, columns - lent), jnp.bfloat16),
-            pltpu.VMEM((n_ga * depth, lent), jnp.bfloat16),
-            pltpu.VMEM((rows, lent), jnp.float32),
+            pltpu.VMEM((n_ga * depth, columns - sum(widths)), jnp.bfloat16),
+            *(pltpu.VMEM((n_ga * depth, size), jnp.bfloat16) for size in widths),
+            *(pltpu.VMEM((rows, size), jnp.float32) for size in widths),
             pltpu.VMEM((n_ga, 1, columns), jnp.float32),
             dma((line * PIECES,)),
             dma((2 * line,)),
             dma((line,)),
             dma((2,)),
             dma((2,)),
+            dma((8,)),
             dma((4,)),
-            dma((2,)),
             dma((n_ba,)),
             dma((2,)),
             dma((3 * GIVEN,)),
             dma((3,)),
+            dma((2,)),
+            dma((2,)),
             dma((1,)),
             dma((1,)),
-            dma((1,)),
-            dma((1,)),
-            dma((3,)),
+            dma((4,)),
         ], 59 * 2**20
 
     def plain(rows, width, depth, columns):

time: 183 us -> 180 us (0.984)
  Pallas kernels: 180 us -> 177 us
    pallas_call x1, Pallas kernels: 180 us -> 177 us  [body(): pl.pallas_call(run, out_shape=(pltpu.VMEM((rows, columns), jnp.bfloat16 i...]
where the time goes in v3:
time: 180 us
  Pallas kernels  177 us (98%)
  local copies, waits for them, and re-layouts  1.93 us (1%)
    pallas_call x1, Pallas kernels, body(): pl.pallas_call(run, out_shape=(pltpu.VMEM((rows, columns), jnp.bfloat16 i...  177 us

profile of v3, /device:TPU:0, one launch (start us, length us, event | category | flops | bytes accessed | tf_op | source)
XLA Modules:
  0.0 180.1 jit_solution(10117218752496676967)
XLA Ops:
  0.6 176.9 %shard_map.41 = (bf16[1280,1536]{1,0:T(8,128)(2,1)S(1)}, f32[1,1536]{1,0:T(1,128)S(1)}) custom-call(bf16[1280,1536]{1,0:T(8,128)(2,1)} %coef.1, bf16[768,1536]{1,0:T(8,128)(2,1)} %rot.1), custom_call_target="tpu_custom_call" | custom-call | tf_op jit(solution)/shard_map/pallas_call | solution.py:844
  177.6 1.9 %copy.5 = bf16[1280,1536]{1,0:T(8,128)(2,1)} copy(bf16[1280,1536]{1,0:T(8,128)(2,1)S(1)} %get-tuple-element.6) | data formatting | bytes 7864320
  179.5 0.6 reduce
